TPU v7x, 32 devices: a whole 2x2x4 slice. The times are simulated.
32 devices in a mesh: slab: 8 (over z, y), chan: 4 (over x, core).
Axes of the slice: x: 2, y: 2, z: 4, core: 2. Of those that a mesh axis runs over, the one named last changes fastest.
Arguments:
- saved_input: float32 [512, 48, 256], P('chan', 'slab'), may hold values from -6 to 6
- pre_first: float32 [512, 48, 256], P('chan', 'slab'), may hold values from -8 to 8
- pre_second: float32 [512, 48, 256], P('chan', 'slab'), may hold values from -8 to 8
- out_grad: float32 [512, 48, 256], P('chan', 'slab'), may hold values from -12 to 12
- weight_first: float32 [27, 512, 512], P(None, 'chan'), may hold values from -0.0546875 to 0.0546875
- weight_second: float32 [27, 512, 512], P(None, 'chan'), may hold values from -0.0546875 to 0.0546875
Outputs:
- input_grad: float32 [512, 48, 256], P('chan', 'slab')
- grad_weight_first: float32 [27, 512, 512], P(None, 'chan', 'slab')
- grad_weight_second: float32 [27, 512, 512], P(None, 'chan', 'slab')
All inputs are finite; a program needn't handle non-finite values.
Results may differ from a plain program's by a relative error of at most 0.00013.
Values sent between devices are 32-bit elements; how exact they have to be, the bound alone decides.
A program may use at most 320 MiB of HBM per device.

v0:
```python
import math

import jax
import jax.numpy as jnp
from jax import lax
from jax.sharding import PartitionSpec as P

OFFSETS = [
    (depth_step, row_step, col_step)
    for depth_step in (-1, 0, 1)
    for row_step in (-1, 0, 1)
    for col_step in (-1, 0, 1)
]


def extended(value, sides, width):
    for axis, dim in sides:
        count, length = (lax.axis_size(axis), value.shape[dim])
        up = [(i, (i + 1) % count) for i in range(count - 1)]
        down = [(j, i) for i, j in up]
        last = lax.slice_in_dim(value, length - width, length, axis=dim)
        initial = lax.slice_in_dim(value, 0, width, axis=dim)
        before = lax.ppermute(last, axis, up)
        after = lax.ppermute(initial, axis, down)
        value = jnp.concatenate([before, value, after], axis=dim)
    return value


def silu_slope(values):
    sigma = jax.nn.sigmoid(values)
    return sigma * (1.0 + values * (1.0 - sigma))


def shift_cells(block, row_step, col_step, side_len):
    area_cells = block.shape[-1]
    if row_step == 0 and col_step == 0:
        return block
    cell_ids = lax.iota(jnp.int32, area_cells)
    row_ids = cell_ids // side_len
    col_ids = cell_ids % side_len
    valid = (
        (row_ids + row_step >= 0)
        & (row_ids + row_step < side_len)
        & (col_ids + col_step >= 0)
        & (col_ids + col_step < side_len)
    )
    rolled = jnp.roll(block, -(row_step * side_len + col_step), axis=-1)
    return jnp.where(valid, rolled, jnp.zeros_like(rolled))


def shifted_inputs(rimmed, planes, side_len):
    pieces = [
        shift_cells(
            rimmed[:, 1 + depth_step : 1 + depth_step + planes, :], row_step, col_step, side_len
        )
        for depth_step, row_step, col_step in OFFSETS
    ]
    stacked = jnp.stack(pieces, 0)
    return stacked.reshape(len(OFFSETS) * rimmed.shape[0], planes * rimmed.shape[2])


def spread_back(summed, channels, planes, side_len):
    area_cells = side_len * side_len
    spread_grid = summed.reshape(len(OFFSETS), channels, planes + 2, area_cells)
    result = jnp.zeros((channels, planes, area_cells), jnp.float32)
    for tap_index, (depth_step, row_step, col_step) in enumerate(OFFSETS):
        result = result + shift_cells(
            spread_grid[tap_index, :, 1 - depth_step : 1 - depth_step + planes, :],
            -row_step,
            -col_step,
            side_len,
        )
    return result


def contract_cells(stacked, grads):
    return lax.dot_general(
        stacked,
        grads,
        (((1,), (1,)), ((), ())),
        precision=lax.Precision.HIGHEST,
        preferred_element_type=jnp.float32,
    )


def back_layer(layer_input, grad_out, weight):
    channels, planes, area_cells = layer_input.shape
    side_len = math.isqrt(area_cells)
    total_out = weight.shape[2]
    tap_rows = weight.reshape(len(OFFSETS) * channels, total_out)
    rimmed_input, rimmed_grad = (
        extended(layer_input, (("slab", 1),), 1),
        extended(grad_out, (("slab", 1),), 1),
    )
    stacked = shifted_inputs(rimmed_input, planes, side_len)
    portion = lax.all_gather(rimmed_grad, "chan", axis=0, tiled=True)
    number = portion.shape[0]
    summed = jnp.dot(
        tap_rows,
        portion.reshape(number, -1),
        precision=lax.Precision.HIGHEST,
        preferred_element_type=jnp.float32,
    )
    centre = portion[:, 1 : planes + 1, :].reshape(number, planes * area_cells)
    products = contract_cells(stacked, centre)
    weight_part = products
    summed, weight_part = (summed, weight_part)
    grad_in = spread_back(summed, channels, planes, side_len)
    voxels = planes * lax.axis_size("slab") * area_cells
    weight_part = weight_part.reshape(len(OFFSETS), channels, total_out) / math.sqrt(voxels)
    return (grad_in, weight_part)


def reduce_layer(weight_part):
    return lax.psum_scatter(weight_part, "slab", scatter_dimension=2, tiled=True)


def per_device(saved_input, pre_first, pre_second, out_grad, weight_first, weight_second):
    hidden = jax.nn.silu(pre_first)
    second_grad = out_grad * silu_slope(pre_second)
    hidden_grad, second_part = back_layer(hidden, second_grad, weight_second)
    second_part = reduce_layer(second_part)
    first_grad = hidden_grad * silu_slope(pre_first)
    input_grad, first_part = back_layer(saved_input, first_grad, weight_first)
    first_weights = reduce_layer(first_part)
    return (input_grad, first_weights, second_part)


def solution(mesh):
    in_specs = (
        P("chan", "slab", None),
        P("chan", "slab", None),
        P("chan", "slab", None),
        P("chan", "slab", None),
        P(None, "chan", None),
        P(None, "chan", None),
    )
    out_specs = (P("chan", "slab", None), P(None, "chan", "slab"), P(None, "chan", "slab"))
    return jax.shard_map(
        per_device, mesh=mesh, in_specs=in_specs, out_specs=out_specs, check_vma=False
    )
```

profile of v0, /device:TPU:22, one launch (start us, length us, event | category | flops | bytes accessed | tf_op | source)
XLA Modules:
  0.0 866.7 jit_solution(14296137979514644748)
XLA Ops:
  8.7 3.4 collective-permute-start.6
  16.2 4.3 collective-permute-start.4
  24.7 3.3 collective-permute-start.1
  87.0 5.4 copy.252
  92.3 53.2 %convolution_bitcast_fusion.1 = f32[3456,2048]{0,1:T(8,128)} fusion(f32[512,2048]{0,1:T(8,128)} %bitcast.447, f32[3456,512]{1,0:T(8,128)} %bitcast.448), kind=kOutput, calls=%fused_computation.1 | convolution fusion | flops 43486543872 | bytes 39583744 | tf_op jit(solution)/shard_map/dot_general | solution.py:98
  145.5 32.4 %reshape.1436 = f32[27,128,8,256]{1,0,3,2:T(8,128)} reshape(f32[3456,2048]{0,1:T(8,128)} %convolution_bitcast_fusion.1) | data formatting | bytes 56623104 | tf_op jit(solution)/shard_map/reshape | solution.py:64
  177.9 48.9 %fusion.178 = (f32[1,128,6,256]{1,0,3,2:T(1,128)}, f32[1,128,6,256]{1,0,3,2:T(1,128)}, f32[1,128,6,256]{1,0,3,2:T(1,128)}, f32[1,128,6,256]{1,0,3,2:T(1,128)}, f...) fusion(f32[27,128,8,256]{1,0,3,2:T(8,128)} %reshape.1436), kind=kLoop, calls=%fused_computation.444 | loop fusion | bytes 29884416 | tf_op jit(solution)/shard_map/slice | solution.py:68
  226.8 3.0 copy.380
  234.0 3.0 copy.389
  241.0 3.0 copy.390
  248.1 3.0 copy.391
  255.2 3.0 copy.392
  262.3 3.0 copy.398
  269.4 3.0 copy.399
  290.7 23.0 %fusion.179 = (f32[1,128,6,256]{1,0,3,2:T(1,128)}, f32[1,128,6,256]{1,0,3,2:T(1,128)}, f32[1,128,6,256]{1,0,3,2:T(1,128)}, f32[1,128,6,256]{1,0,3,2:T(1,128)}, f...) fusion(f32[27,128,8,256]{1,0,3,2:T(8,128)} %reshape.1436), kind=kLoop, calls=%fused_computation.445 | loop fusion | bytes 12582912 | tf_op jit(solution)/shard_map/slice | solution.py:68
  327.8 3.0 copy.383
  344.7 3.0 copy.395
  349.7 3.2 copy.396
  359.7 3.0 copy.403
  374.5 3.0 copy.393
  395.3 3.0 copy.406
  400.2 3.0 copy.384
  403.2 12.3 %fusion.68 = f32[128,6,256]{2,0,1:T(8,128)S(1)} fusion(f32[128,6,240]{2,0,1:T(8,128)} %bitcast.437, f32[128,6,16]{2,0,1:T(8,128)} %slice.1228, f32[128,6,239]{2,0,1:T(8,128)} %bitcast.445, f32[128,6,17]{2,0,1:T(8,128)} %slice.1231, f32[128,6,256]{2,0,1:T(8,128)} %param.7, f32[128,6,241]{2,0,1:T(8,128)} %bitcast.433, f32[128,6,15]{2,0,1:T(8,128)} %slice.1225, ...), kind=kLoop, calls=%fused_computation.189 | loop fusion | flops 16121856 | bytes 22808576 | tf_op jit(solution)/shard_map/mul | solution.py:123
  415.6 3.4 collective-permute-start.2
  422.5 4.3 collective-permute-done.3
  428.2 3.4 fusion.130
  432.6 3.1 bitcast_dynamic-update-slice_fusion
  435.7 3.5 fusion.131
  439.3 3.2 fusion.132
  442.5 3.2 fusion.133
  445.8 3.1 fusion.134
  464.4 49.6 %bitcast_multiply_fusion = f32[27,128,512]{1,2,0:T(8,128)} fusion(f32[27,128,6,256]{3,1,2,0:T(8,128)} %get-tuple-element.179, f32[512,6,256,1]{2,0,1,3:T(8,128)S(1)} %slice_bitcast_fusion.76), kind=kOutput, calls=%fused_computation.2 | convolution fusion | flops 32616677376 | bytes 31457280 | tf_op jit(solution)/shard_map/dot_general | solution.py:77
  516.0 5.8 collective-permute-done.5
  536.0 48.3 %bitcast_multiply_fusion.1 = f32[27,128,512]{1,2,0:T(8,128)} fusion(f32[27,128,6,256]{3,1,2,0:T(8,128)} %fusion.118, f32[512,6,256,1]{2,0,1,3:T(8,128)S(1)} %slice_bitcast_fusion.77), kind=kOutput, calls=%fused_computation.3 | convolution fusion | flops 32616677376 | bytes 31457280 | tf_op jit(solution)/shard_map/dot_general | solution.py:77
  584.3 5.4 copy.281
  589.7 53.1 %convolution_bitcast_fusion = f32[3456,2048]{0,1:T(8,128)} fusion(f32[512,2048]{0,1:T(8,128)} %bitcast.446, f32[3456,512]{1,0:T(8,128)} %bitcast.449), kind=kOutput, calls=%fused_computation | convolution fusion | flops 43486543872 | bytes 39583744 | tf_op jit(solution)/shard_map/dot_general | solution.py:98
  642.8 32.6 %reshape.1437 = f32[27,128,8,256]{1,0,3,2:T(8,128)} reshape(f32[3456,2048]{0,1:T(8,128)} %convolution_bitcast_fusion) | data formatting | bytes 56623104 | tf_op jit(solution)/shard_map/reshape | solution.py:64
  675.4 48.8 %fusion.176 = (f32[1,128,6,256]{1,0,3,2:T(1,128)}, f32[1,128,6,256]{1,0,3,2:T(1,128)}, f32[1,128,6,256]{1,0,3,2:T(1,128)}, f32[1,128,6,256]{1,0,3,2:T(1,128)}, f...) fusion(f32[27,128,8,256]{1,0,3,2:T(8,128)} %reshape.1437), kind=kLoop, calls=%fused_computation.442 | loop fusion | bytes 29884416 | tf_op jit(solution)/shard_map/slice | solution.py:68
  756.3 22.7 %fusion.177 = (f32[1,128,6,256]{1,0,3,2:T(1,128)S(1)}, f32[1,128,6,256]{1,0,3,2:T(1,128)}, f32[1,128,6,256]{1,0,3,2:T(1,128)}, f32[1,128,6,256]{1,0,3,2:T(1,128)...) fusion(f32[27,128,8,256]{1,0,3,2:T(8,128)} %reshape.1437), kind=kLoop, calls=%fused_computation.443 | loop fusion | bytes 12582912 | tf_op jit(solution)/shard_map/slice | solution.py:68
  803.8 3.2 copy.430
  808.9 3.0 copy.431
  821.8 3.0 copy.429
  824.8 3.0 copy.412
  829.8 3.0 copy.413
  834.7 3.0 copy.414
  839.7 3.0 copy.433
  844.6 3.0 copy.411
  847.6 12.1 %fusion.94 = f32[128,6,256]{2,0,1:T(8,128)} fusion(f32[128,6,240]{2,0,1:T(8,128)} %bitcast.413, f32[128,6,16]{2,0,1:T(8,128)} %slice.1305, f32[128,6,239]{2,0,1:T(8,128)} %bitcast.435, f32[128,6,17]{2,0,1:T(8,128)} %slice.1308, f32[128,6,241]{2,0,1:T(8,128)} %bitcast.411, f32[128,6,15]{2,0,1:T(8,128)} %slice.1302, f32[128,6,255]{2,0,1:T(8,128)} %bitcast.409, ...), kind=kLoop, calls=%fused_computation.239 | loop fusion | flops 14548992 | bytes 22022144 | tf_op jit(solution)/shard_map/add | solution.py:67
  (295 shorter events, 293.0 us)
Async XLA Ops:
  7.2 38.4 %copy-start = (f32[128,6,256]{2,0,1:T(8,128)S(1)}, f32[128,6,256]{2,0,1:T(8,128)}, u32[]{:S(2)}) copy-start(f32[128,6,256]{2,0,1:T(8,128)} %param.6) | copy-start | bytes 2359300
  7.2 79.8 %all-gather.3.cloned.1.call-start = ((), (), s32[]{:S(2)}) async-start(), calls=%async_computation.2 | async-start | bytes 5242880 | tf_op jit(solution)/shard_map/all_gather | solution.py:96
  8.7 40.2 %collective-permute-start.6 = (f32[128,1,256]{2,0,1:T(8,128)S(1)}, f32[128,1,256]{2,0,1:T(8,128)S(1)}, u32[]{:S(2)}, u32[]{:S(2)}) collective-permute-start(f32[128,1,256]{2,0,1:T(8,128)S(1)} %get-tuple-element.154), channel_id=1, source_target_pairs={{0,4},{4,8},{8,12},{12,16},{16,20},{20,24},{24,28},{1,5},{5,9},{9,... | collective-permute-start | bytes 393224 | tf_op jit(solution)/shard_map/ppermute | solution.py:23
  12.1 36.8 %collective-permute-start.7 = (f32[128,1,256]{2,0,1:T(8,128)S(1)}, f32[128,1,256]{2,0,1:T(8,128)S(1)}, u32[]{:S(2)}, u32[]{:S(2)}) collective-permute-start(f32[128,1,256]{2,0,1:T(8,128)S(1)} %get-tuple-element.153), channel_id=1, source_target_pairs={{4,0},{8,4},{12,8},{16,12},{20,16},{24,20},{28,24},{5,1},{9,5},{13... | collective-permute-start | bytes 393224 | tf_op jit(solution)/shard_map/ppermute | solution.py:24
  16.2 39.6 %collective-permute-start.4 = (f32[128,1,256]{2,0,1:T(8,128)S(1)}, f32[128,1,256]{2,0,1:T(8,128)}, u32[]{:S(2)}, u32[]{:S(2)}) collective-permute-start(f32[128,1,256]{2,0,1:T(8,128)S(1)} %get-tuple-element.156), channel_id=1, source_target_pairs={{0,4},{4,8},{8,12},{12,16},{16,20},{20,24},{24,28},{1,5},{5,9},{9,... | collective-permute-start | bytes 393224 | tf_op jit(solution)/shard_map/ppermute | solution.py:23
  22.2 25.6 %collective-permute-start = (f32[128,1,256]{2,0,1:T(8,128)S(1)}, f32[128,1,256]{2,0,1:T(8,128)S(1)}, u32[]{:S(2)}, u32[]{:S(2)}) collective-permute-start(f32[128,1,256]{2,0,1:T(8,128)S(1)} %get-tuple-element.177), channel_id=1, source_target_pairs={{0,4},{4,8},{8,12},{12,16},{16,20},{20,24},{24,28},{1,5},{5,9},{9,... | collective-permute-start | bytes 393224 | tf_op jit(solution)/shard_map/ppermute | solution.py:23
  24.7 23.0 %collective-permute-start.1 = (f32[128,1,256]{2,0,1:T(8,128)S(1)}, f32[128,1,256]{2,0,1:T(8,128)S(1)}, u32[]{:S(2)}, u32[]{:S(2)}) collective-permute-start(f32[128,1,256]{2,0,1:T(8,128)S(1)} %get-tuple-element.178), channel_id=1, source_target_pairs={{4,0},{8,4},{12,8},{16,12},{20,16},{24,20},{28,24},{5,1},{9,5},{13... | collective-permute-start | bytes 393224 | tf_op jit(solution)/shard_map/ppermute | solution.py:24
  48.8 484.8 %all-gather.5.cloned.1.call-start = ((), (), s32[]{:S(2)}) async-start(), calls=%async_computation.3 | async-start | bytes 5242880 | tf_op jit(solution)/shard_map/all_gather | solution.py:96
  415.6 6.9 collective-permute-start.2
  419.0 7.8 collective-permute-start.3
  427.9 431.8 %reduce-scatter.5.cloned.1.call-start = ((), (), s32[]{:S(2)}) async-start(), calls=%async_computation.5 | async-start | bytes 7962624 | tf_op jit(solution)/shard_map/reduce_scatter | solution.py:115
  428.0 20.9 %copy-start.5 = (f32[1,128,6,239]{3,1,2,0:T(8,128)S(1)}, f32[1,128,6,239]{3,1,2,0:T(8,128)}, u32[]{:S(2)}) copy-start(f32[1,128,6,239]{3,1,2,0:T(8,128)} %get-tuple-element.58) | copy-start | bytes 2202628
  428.0 20.9 %copy-start.17 = (f32[1,128,6,239]{3,1,2,0:T(8,128)S(1)}, f32[1,128,6,239]{3,1,2,0:T(8,128)}, u32[]{:S(2)}) copy-start(f32[1,128,6,239]{3,1,2,0:T(8,128)} %get-tuple-element.160) | copy-start | bytes 2202628
  428.0 22.5 %copy-start.6 = (f32[1,128,6,240]{3,1,2,0:T(8,128)S(1)}, f32[1,128,6,240]{3,1,2,0:T(8,128)}, u32[]{:S(2)}) copy-start(f32[1,128,6,240]{3,1,2,0:T(8,128)} %get-tuple-element.62) | copy-start | bytes 2211844
  428.0 22.5 %copy-start.16 = (f32[1,128,6,240]{3,1,2,0:T(8,128)S(1)}, f32[1,128,6,240]{3,1,2,0:T(8,128)}, u32[]{:S(2)}) copy-start(f32[1,128,6,240]{3,1,2,0:T(8,128)} %get-tuple-element.164) | copy-start | bytes 2211844
  428.0 22.5 %copy-start.23 = (f32[1,128,6,16]{3,1,2,0:T(8,128)S(1)}, f32[1,128,6,16]{3,1,2,0:T(8,128)}, u32[]{:S(2)}) copy-start(f32[1,128,6,16]{3,1,2,0:T(8,128)} %get-tuple-element.64) | copy-start | bytes 147460
  428.0 22.5 %copy-start.32 = (f32[1,128,6,16]{3,1,2,0:T(8,128)S(1)}, f32[1,128,6,16]{3,1,2,0:T(8,128)}, u32[]{:S(2)}) copy-start(f32[1,128,6,16]{3,1,2,0:T(8,128)} %get-tuple-element.166) | copy-start | bytes 147460
  428.1 24.2 %copy-start.8 = (f32[1,128,6,241]{3,1,2,0:T(8,128)S(1)}, f32[1,128,6,241]{3,1,2,0:T(8,128)}, u32[]{:S(2)}) copy-start(f32[1,128,6,241]{3,1,2,0:T(8,128)} %get-tuple-element.66) | copy-start | bytes 2221060
  428.1 24.2 %copy-start.15 = (f32[1,128,6,241]{3,1,2,0:T(8,128)S(1)}, f32[1,128,6,241]{3,1,2,0:T(8,128)}, u32[]{:S(2)}) copy-start(f32[1,128,6,241]{3,1,2,0:T(8,128)} %get-tuple-element.168) | copy-start | bytes 2221060
  428.1 24.2 %copy-start.24 = (f32[1,128,6,15]{3,1,2,0:T(8,128)S(1)}, f32[1,128,6,15]{3,1,2,0:T(8,128)}, u32[]{:S(2)}) copy-start(f32[1,128,6,15]{3,1,2,0:T(8,128)} %get-tuple-element.68) | copy-start | bytes 138244
  428.1 24.2 %copy-start.31 = (f32[1,128,6,15]{3,1,2,0:T(8,128)S(1)}, f32[1,128,6,15]{3,1,2,0:T(8,128)}, u32[]{:S(2)}) copy-start(f32[1,128,6,15]{3,1,2,0:T(8,128)} %get-tuple-element.170) | copy-start | bytes 138244
  428.1 25.9 %copy-start.9 = (f32[1,128,6,255]{3,1,2,0:T(8,128)S(1)}, f32[1,128,6,255]{3,1,2,0:T(8,128)}, u32[]{:S(2)}) copy-start(f32[1,128,6,255]{3,1,2,0:T(8,128)} %get-tuple-element.70) | copy-start | bytes 2350084
  428.1 25.8 %copy-start.14 = (f32[1,128,6,255]{3,1,2,0:T(8,128)S(1)}, f32[1,128,6,255]{3,1,2,0:T(8,128)}, u32[]{:S(2)}) copy-start(f32[1,128,6,255]{3,1,2,0:T(8,128)} %get-tuple-element.172) | copy-start | bytes 2350084
  428.1 25.8 %copy-start.25 = (f32[1,128,6,1]{3,1,2,0:T(8,128)S(1)}, f32[1,128,6,1]{3,1,2,0:T(8,128)}, u32[]{:S(2)}) copy-start(f32[1,128,6,1]{3,1,2,0:T(8,128)} %get-tuple-element.72) | copy-start | bytes 9220
  428.1 25.8 %copy-start.30 = (f32[1,128,6,1]{3,1,2,0:T(8,128)S(1)}, f32[1,128,6,1]{3,1,2,0:T(8,128)}, u32[]{:S(2)}) copy-start(f32[1,128,6,1]{3,1,2,0:T(8,128)} %get-tuple-element.174) | copy-start | bytes 9220
  428.1 29.4 %copy-start.7 = (f32[1,128,6,255]{3,1,2,0:T(8,128)S(1)}, f32[1,128,6,255]{3,1,2,0:T(8,128)}, u32[]{:S(2)}) copy-start(f32[1,128,6,255]{3,1,2,0:T(8,128)} %get-tuple-element.69) | copy-start | bytes 2350084
  428.1 29.4 %copy-start.13 = (f32[1,128,6,255]{3,1,2,0:T(8,128)S(1)}, f32[1,128,6,255]{3,1,2,0:T(8,128)}, u32[]{:S(2)}) copy-start(f32[1,128,6,255]{3,1,2,0:T(8,128)} %get-tuple-element.171) | copy-start | bytes 2350084
  428.2 29.3 %copy-start.22 = (f32[1,128,6,1]{3,1,2,0:T(8,128)S(1)}, f32[1,128,6,1]{3,1,2,0:T(8,128)}, u32[]{:S(2)}) copy-start(f32[1,128,6,1]{3,1,2,0:T(8,128)} %get-tuple-element.71) | copy-start | bytes 9220
  428.2 29.3 %copy-start.29 = (f32[1,128,6,1]{3,1,2,0:T(8,128)S(1)}, f32[1,128,6,1]{3,1,2,0:T(8,128)}, u32[]{:S(2)}) copy-start(f32[1,128,6,1]{3,1,2,0:T(8,128)} %get-tuple-element.173) | copy-start | bytes 9220
  431.5 28.0 %copy-start.4 = (f32[1,128,6,241]{3,1,2,0:T(8,128)S(1)}, f32[1,128,6,241]{3,1,2,0:T(8,128)}, u32[]{:S(2)}) copy-start(f32[1,128,6,241]{3,1,2,0:T(8,128)} %get-tuple-element.65) | copy-start | bytes 2221060
  431.5 28.0 %copy-start.12 = (f32[1,128,6,241]{3,1,2,0:T(8,128)S(1)}, f32[1,128,6,241]{3,1,2,0:T(8,128)}, u32[]{:S(2)}) copy-start(f32[1,128,6,241]{3,1,2,0:T(8,128)} %get-tuple-element.167) | copy-start | bytes 2221060
  431.5 28.0 %copy-start.20 = (f32[1,128,6,15]{3,1,2,0:T(8,128)S(1)}, f32[1,128,6,15]{3,1,2,0:T(8,128)}, u32[]{:S(2)}) copy-start(f32[1,128,6,15]{3,1,2,0:T(8,128)} %get-tuple-element.67) | copy-start | bytes 138244
  431.6 28.0 %copy-start.28 = (f32[1,128,6,15]{3,1,2,0:T(8,128)S(1)}, f32[1,128,6,15]{3,1,2,0:T(8,128)}, u32[]{:S(2)}) copy-start(f32[1,128,6,15]{3,1,2,0:T(8,128)} %get-tuple-element.169) | copy-start | bytes 138244
  431.6 28.0 %copy-start.38 = (pred[256]{0:T(512)(128)(4,1)S(1)}, pred[256]{0:T(512)(128)(4,1)}, u32[]{:S(2)}) copy-start(pred[256]{0:T(512)(128)(4,1)} %get-tuple-element.216) | copy-start | bytes 772
  435.7 25.4 %copy-start.3 = (f32[1,128,6,240]{3,1,2,0:T(8,128)S(1)}, f32[1,128,6,240]{3,1,2,0:T(8,128)}, u32[]{:S(2)}) copy-start(f32[1,128,6,240]{3,1,2,0:T(8,128)} %get-tuple-element.61) | copy-start | bytes 2211844
  435.7 25.4 %copy-start.11 = (f32[1,128,6,240]{3,1,2,0:T(8,128)S(1)}, f32[1,128,6,240]{3,1,2,0:T(8,128)}, u32[]{:S(2)}) copy-start(f32[1,128,6,240]{3,1,2,0:T(8,128)} %get-tuple-element.163) | copy-start | bytes 2211844
  435.7 25.4 %copy-start.19 = (f32[1,128,6,16]{3,1,2,0:T(8,128)S(1)}, f32[1,128,6,16]{3,1,2,0:T(8,128)}, u32[]{:S(2)}) copy-start(f32[1,128,6,16]{3,1,2,0:T(8,128)} %get-tuple-element.63) | copy-start | bytes 147460
  435.7 25.4 %copy-start.27 = (f32[1,128,6,16]{3,1,2,0:T(8,128)S(1)}, f32[1,128,6,16]{3,1,2,0:T(8,128)}, u32[]{:S(2)}) copy-start(f32[1,128,6,16]{3,1,2,0:T(8,128)} %get-tuple-element.165) | copy-start | bytes 147460
  435.7 25.4 %copy-start.41 = (pred[256]{0:T(512)(128)(4,1)S(1)}, pred[256]{0:T(512)(128)(4,1)}, u32[]{:S(2)}) copy-start(pred[256]{0:T(512)(128)(4,1)} %get-tuple-element.217) | copy-start | bytes 772
  439.2 23.4 %copy-start.2 = (f32[1,128,6,239]{3,1,2,0:T(8,128)S(1)}, f32[1,128,6,239]{3,1,2,0:T(8,128)}, u32[]{:S(2)}) copy-start(f32[1,128,6,239]{3,1,2,0:T(8,128)} %get-tuple-element.57) | copy-start | bytes 2202628
  439.3 23.4 %copy-start.10 = (f32[1,128,6,239]{3,1,2,0:T(8,128)S(1)}, f32[1,128,6,239]{3,1,2,0:T(8,128)}, u32[]{:S(2)}) copy-start(f32[1,128,6,239]{3,1,2,0:T(8,128)} %get-tuple-element.159) | copy-start | bytes 2202628
  439.3 23.4 %copy-start.18 = (f32[1,128,6,17]{3,1,2,0:T(8,128)S(1)}, f32[1,128,6,17]{3,1,2,0:T(8,128)}, u32[]{:S(2)}) copy-start(f32[1,128,6,17]{3,1,2,0:T(8,128)} %get-tuple-element.59) | copy-start | bytes 156676
  439.3 23.4 %copy-start.26 = (f32[1,128,6,17]{3,1,2,0:T(8,128)S(1)}, f32[1,128,6,17]{3,1,2,0:T(8,128)}, u32[]{:S(2)}) copy-start(f32[1,128,6,17]{3,1,2,0:T(8,128)} %get-tuple-element.161) | copy-start | bytes 156676
  439.3 23.4 %copy-start.43 = (pred[256]{0:T(512)(128)(4,1)S(1)}, pred[256]{0:T(512)(128)(4,1)}, u32[]{:S(2)}) copy-start(pred[256]{0:T(512)(128)(4,1)} %get-tuple-element.218) | copy-start | bytes 772
  442.5 21.7 %copy-start.1 = (f32[512,8,256]{2,0,1:T(8,128)S(1)}, f32[512,8,256]{2,0,1:T(8,128)}, u32[]{:S(2)}) copy-start(f32[512,8,256]{2,0,1:T(8,128)} %all-gather.3.cloned.1.call-done) | copy-start | bytes 12582916
  464.4 49.7 %copy-start.34 = (f32[128,1,256]{2,0,1:T(8,128)S(1)}, f32[128,1,256]{2,0,1:T(8,128)}, u32[]{:S(2)}) copy-start(f32[128,1,256]{2,0,1:T(8,128)} %get-tuple-element.155) | copy-start | bytes 393220
  514.0 345.7 %reduce-scatter.3.cloned.1.call-start = ((), (), s32[]{:S(2)}) async-start(), calls=%async_computation.4 | async-start | bytes 7962624 | tf_op jit(solution)/shard_map/reduce_scatter | solution.py:115
  514.1 7.8 collective-permute-start.5
  (8 other events, 140.1 us)
Sparse Core Ops, SparseCore 0:
  48.9 33.5 all-gather.2
  428.0 33.5 all-gather.4
  514.1 128.6 reduce-scatter.4
  647.0 128.6 reduce-scatter.2
where the time goes:
time: 881 us; the launch traced here: 867 us
  local copies, waits for them, and re-layouts  510 us (58%)
  matrix products  204 us (23%)
  other arithmetic  103 us (12%)
  starting transfers between devices  23.9 us (3%)
  between operations  15 us (2%)
  waiting for transfers between devices  10.3 us (1%)
    unnamed x147, local copies, waits for them, and re-layouts  144 us
    slice x4, local copies, waits for them, and re-layouts, spread_back(): spread_grid[tap_index, :, 1 - depth_step:1 - depth_step + planes, :]  143 us
    slice x72, local copies, waits for them, and re-layouts, shift_cells(): rolled = jnp.roll(block, -(row_step * side_len + col_step), axis=-1)  114 us
    dot_general x2, matrix products, back_layer(): jnp.dot(tap_rows, portion.reshape(number, -1), precision=lax.Precision.HI...  106 us
    dot_general x2, matrix products, contract_cells(): lax.dot_general(stacked, grads, (((1,), (1,)), ((), ())), precision=lax.P...  97.9 us
    reshape x2, local copies, waits for them, and re-layouts, spread_back(): spread_grid = summed.reshape(len(OFFSETS), channels, planes + 2, area_cells)  65 us
    unnamed x33, other arithmetic  55.2 us
    concatenate x24, local copies, waits for them, and re-layouts, shift_cells(): rolled = jnp.roll(block, -(row_step * side_len + col_step), axis=-1)  28.9 us
  transfers between devices with their start and end apart: 12, of which 2 were waited for; matrix products, arithmetic and copies ran while one was open for 56% of the time, Pallas kernels for 0%

commit v1 on v0

v1 whole, which is shorter than its diff:
```python
import math

import jax
import jax.numpy as jnp
from jax import lax
from jax.sharding import PartitionSpec as P

STEPS = (-1, 0, 1)
IN_PLANE = [(row_step, col_step) for row_step in STEPS for col_step in STEPS]


def with_rim(value):
    count = lax.axis_size("slab")
    up = [(i, i + 1) for i in range(count - 1)]
    down = [(j, i) for i, j in up]
    before = lax.ppermute(value[-1:], "slab", up)
    after = lax.ppermute(value[:1], "slab", down)
    return jnp.concatenate([before, value, after], axis=0)


def silu_slope(values):
    sigma = jax.nn.sigmoid(values)
    return sigma * (1.0 + values * (1.0 - sigma))


def shift_cells(block, row_step, col_step, side_len):
    area_cells = block.shape[-1]
    if row_step == 0 and col_step == 0:
        return block
    cell_ids = lax.iota(jnp.int32, area_cells)
    row_ids = cell_ids // side_len
    col_ids = cell_ids % side_len
    valid = (
        (row_ids + row_step >= 0)
        & (row_ids + row_step < side_len)
        & (col_ids + col_step >= 0)
        & (col_ids + col_step < side_len)
    )
    rolled = jnp.roll(block, -(row_step * side_len + col_step), axis=-1)
    return jnp.where(valid, rolled, jnp.zeros_like(rolled))


def gather_channels(rimmed):
    planes, channels, cells = rimmed.shape
    portion = lax.all_gather(rimmed, "chan", axis=0)
    return portion.transpose(1, 0, 2, 3).reshape(planes, -1, cells)


def input_side(portion, weight, side_len):
    planes = portion.shape[0] - 2
    channels, total = weight.shape[1:]
    near = jnp.stack([portion[1 - a : 1 - a + planes] for a in STEPS], 0)
    rows = weight.reshape(len(STEPS), len(IN_PLANE) * channels, total)
    summed = lax.dot_general(
        rows,
        near,
        (((0, 2), (0, 2)), ((), ())),
        precision=lax.Precision.HIGH,
        preferred_element_type=jnp.float32,
    )
    summed = summed.reshape(len(IN_PLANE), channels, planes, -1)
    result = jnp.zeros(summed.shape[1:], jnp.float32)
    for index, (row_step, col_step) in enumerate(IN_PLANE):
        result = result + shift_cells(summed[index], -row_step, -col_step, side_len)
    return result.transpose(1, 0, 2)


def weight_side(rimmed, centre, side_len):
    planes, total, cells = centre.shape
    channels = rimmed.shape[1]
    moved = jnp.stack([shift_cells(rimmed, b, c, side_len) for b, c in IN_PLANE], 1)
    moved = moved.reshape(planes + 2, len(IN_PLANE) * channels, cells)
    voxels = planes * lax.axis_size("slab") * cells
    parts = []
    for a in STEPS:
        part = lax.dot_general(
            moved[1 + a : 1 + a + planes],
            centre,
            (((0, 2), (0, 2)), ((), ())),
            precision=lax.Precision.HIGH,
            preferred_element_type=jnp.float32,
        )
        parts.append(part.reshape(len(IN_PLANE), channels, total) / math.sqrt(voxels))
    return parts


def reduce_parts(parts):
    done = [lax.psum_scatter(part, "slab", scatter_dimension=2, tiled=True) for part in parts]
    return jnp.concatenate(done, 0)


def per_device(saved_input, pre_first, pre_second, out_grad, weight_first, weight_second):
    side_len = math.isqrt(saved_input.shape[-1])
    saved_input, pre_first, pre_second, out_grad = (
        value.transpose(1, 0, 2) for value in (saved_input, pre_first, pre_second, out_grad)
    )
    second_grad = out_grad * silu_slope(pre_second)
    second_all = gather_channels(with_rim(second_grad))
    hidden = with_rim(jax.nn.silu(pre_first))
    input_rim = with_rim(saved_input)
    hidden_grad = input_side(second_all, weight_second, side_len)
    first_grad = hidden_grad * silu_slope(pre_first)
    first_all = gather_channels(with_rim(first_grad))
    second_parts = weight_side(hidden, second_all[1:-1], side_len)
    first_all, second_parts = lax.optimization_barrier((first_all, second_parts))
    first_parts = weight_side(input_rim, first_all[1:-1], side_len)
    input_grad = input_side(first_all, weight_first, side_len)
    return (input_grad.transpose(1, 0, 2), reduce_parts(first_parts), reduce_parts(second_parts))


def solution(mesh):
    in_specs = (
        P("chan", "slab", None),
        P("chan", "slab", None),
        P("chan", "slab", None),
        P("chan", "slab", None),
        P(None, "chan", None),
        P(None, "chan", None),
    )
    out_specs = (P("chan", "slab", None), P(None, "chan", "slab"), P(None, "chan", "slab"))
    return jax.shard_map(
        per_device, mesh=mesh, in_specs=in_specs, out_specs=out_specs, check_vma=False
    )
```

time: 881 us -> 784 us (0.89)
  waiting for transfers between devices: 10.3 us -> 444 us
  local copies, waits for them, and re-layouts: 510 us -> 169 us
  matrix products: 204 us -> 99.9 us
  other arithmetic: 103 us -> 25 us
    reduce_scatter x2 -> x6, waiting for transfers between devices: 0.04 us -> 426 us  [reduce_parts(): lax.psum_scatter(part, 'slab', scatter_dimension=2, tiled=True)]
    unnamed x147 -> x47, local copies, waits for them, and re-layouts: 144 us -> 9.79 us
    slice x72 -> x16, local copies, waits for them, and re-layouts: 114 us -> 0.94 us  [shift_cells(): rolled = jnp.roll(block, -(row_step * side_len + col_step), axis=-1)]
    dot_general x4 -> x8, matrix products: 204 us -> 99.9 us  [the longest x6 52.6 us: weight_side(): lax.dot_general(moved[1 + a:1 + a + planes], centre, (((0, 2), (0, 2)), (...]
    reshape x2 -> x1, local copies, waits for them, and re-layouts: 65 us -> 5.45 us  [gather_channels(): return portion.transpose(1, 0, 2, 3).reshape(planes, -1, cells)]
    slice x8 -> x14, local copies, waits for them, and re-layouts: 145 us -> 86.8 us  [the longest x8 77.2 us: weight_side(): moved[1 + a:1 + a + planes]]
    unnamed x33 -> x10, other arithmetic: 55.2 us -> 13.8 us
    concatenate x24 -> x16, local copies, waits for them, and re-layouts: 28.9 us -> 8.24 us  [shift_cells(): rolled = jnp.roll(block, -(row_step * side_len + col_step), axis=-1)]
  transfers between devices with their start and end apart: 12 -> 16, of which waited for: 2 -> 12; matrix products, arithmetic and copies ran while one was open for 56% -> 27% of each run, Pallas kernels for 0% -> 0%
where the time goes in v1:
time: 784 us; the launch traced here: 777 us
  waiting for transfers between devices  444 us (57%)
  local copies, waits for them, and re-layouts  169 us (22%)
  matrix products  99.9 us (13%)
  other arithmetic  25 us (3%)
  starting transfers between devices  23.8 us (3%)
  between operations  15.2 us (2%)
    reduce_scatter x6, waiting for transfers between devices, reduce_parts(): lax.psum_scatter(part, 'slab', scatter_dimension=2, tiled=True)  426 us
    slice x8, local copies, waits for them, and re-layouts, weight_side(): moved[1 + a:1 + a + planes]  77.2 us
    dot_general x6, matrix products, weight_side(): lax.dot_general(moved[1 + a:1 + a + planes], centre, (((0, 2), (0, 2)), (...  52.6 us
    dot_general x2, matrix products, input_side(): lax.dot_general(rows, near, (((0, 2), (0, 2)), ((), ())), precision=lax.P...  47.3 us
    another operation x4, local copies, waits for them, and re-layouts, input_side(): near = jnp.stack([portion[1 - a:1 - a + planes] for a in STEPS], 0)  20.1 us
  transfers between devices with their start and end apart: 16, of which 12 were waited for; matrix products, arithmetic and copies ran while one was open for 27% of the time, Pallas kernels for 0%

profile of v1, /device:TPU:22, one launch (start us, length us, event | category | flops | bytes accessed | tf_op | source)
XLA Modules:
  0.0 776.9 jit_solution(15282233944061165967)
XLA Ops:
  10.4 3.4 collective-permute-start
  13.8 2.4 collective-permute-start.1
  17.5 4.1 collective-permute-done.1
  23.7 3.1 collective-permute-start.4
  26.8 2.8 collective-permute-start.5
  31.1 4.0 collective-permute-start.6
  37.9 4.9 collective-permute-done.7
  56.8 5.4 copy.68
  62.2 6.4 fusion.119
  68.6 5.1 stack.25
  73.7 5.1 stack.24
  78.8 5.0 stack.26
  83.8 23.9 %fusion.27 = f32[1152,6,256]{0,2,1:T(8,128)S(1)} fusion(f32[3,1152,512,1]{2,1,0,3:T(8,128)} %bitcast.263, f32[1,6,512,256]{2,3,0,1:T(8,128)} %stack.26, f32[1,6,512,256]{2,3,0,1:T(8,128)} %stack.25, f32[1,6,512,256]{2,3,0,1:T(8,128)} %stack.24), kind=kOutput, calls=%fused_computation.25 | convolution fusion | flops 16312172544 | bytes 23592960 | tf_op jit(solution)/shard_map/dot_general | solution.py:54
  108.8 1.9 fusion.79
  110.8 3.4 collective-permute-start.2
  114.2 2.5 collective-permute-start.3
  118.3 4.0 collective-permute-done.3
  123.4 2.6 copy.70
  139.5 14.4 %fusion.102 = (f32[6,9,128,256]{2,3,0,1:T(8,128)}, f32[6,9,128,256]{2,3,0,1:T(8,128)}, f32[6,9,128,256]{2,3,0,1:T(8,128)}) fusion(f32[8,9,128,256]{2,3,0,1:T(8,128)} %get-tuple-element.105), kind=kLoop, calls=%fused_computation.190 | loop fusion | bytes 42467328 | tf_op jit(solution)/shard_map/slice | solution.py:77
  153.8 8.0 %copy.77 = f32[6,9,128,256]{3,2,1,0:T(8,128)} copy(f32[6,9,128,256]{2,3,0,1:T(8,128)} %get-tuple-element.23) | data formatting | bytes 14155776 | tf_op jit(solution)/shard_map/slice | solution.py:77
  161.8 8.0 %copy.76 = f32[6,9,128,256]{3,2,1,0:T(8,128)} copy(f32[6,9,128,256]{2,3,0,1:T(8,128)} %get-tuple-element.24) | data formatting | bytes 14155776 | tf_op jit(solution)/shard_map/slice | solution.py:77
  169.8 8.0 %copy.74 = f32[6,9,128,256]{3,2,1,0:T(8,128)} copy(f32[6,9,128,256]{2,3,0,1:T(8,128)} %get-tuple-element.25) | data formatting | bytes 14155776 | tf_op jit(solution)/shard_map/slice | solution.py:77
  177.9 3.1 copy.75
  181.0 9.1 %bitcast_multiply_fusion.3 = f32[9,128,512]{2,1,0:T(8,128)} fusion(f32[6,512,256,1]{2,1,3,0:T(8,128)S(1)} %bitcast.251, f32[6,9,128,256]{3,2,1,0:T(8,128)} %copy.77), kind=kOutput, calls=%fused_computation.38 | convolution fusion | flops 5436407808 | bytes 12582912 | tf_op jit(solution)/shard_map/dot_general | solution.py:76
  190.1 9.5 %bitcast_multiply_fusion.4 = f32[9,128,512]{2,1,0:T(8,128)} fusion(f32[6,512,256,1]{2,1,3,0:T(8,128)S(1)} %bitcast.252, f32[6,9,128,256]{3,2,1,0:T(8,128)} %copy.76), kind=kOutput, calls=%fused_computation.39 | convolution fusion | flops 5436407808 | bytes 12582912 | tf_op jit(solution)/shard_map/dot_general | solution.py:76
  199.6 7.1 bitcast_multiply_fusion.5
  206.8 5.4 copy.71
  212.1 5.4 reshape.545
  217.6 3.4 copy.95
  221.1 5.1 copy.96
  226.3 3.4 copy.97
  229.8 14.4 %fusion.101 = (f32[6,9,128,256]{2,3,0,1:T(8,128)}, f32[6,9,128,256]{2,3,0,1:T(8,128)}, f32[6,9,128,256]{2,3,0,1:T(8,128)}) fusion(f32[8,9,128,256]{2,3,0,1:T(8,128)} %get-tuple-element.104), kind=kLoop, calls=%fused_computation.189 | loop fusion | bytes 42467328 | tf_op jit(solution)/shard_map/slice | solution.py:77
  244.2 8.1 %copy.83 = f32[6,9,128,256]{3,2,1,0:T(8,128)} copy(f32[6,9,128,256]{2,3,0,1:T(8,128)} %get-tuple-element.20) | data formatting | bytes 14155776 | tf_op jit(solution)/shard_map/slice | solution.py:77
  252.4 9.0 %bitcast_multiply_fusion.2 = f32[9,128,512]{2,1,0:T(8,128)S(1)} fusion(f32[8,512,256]{1,2,0:T(8,128)} %reshape.545, f32[6,9,128,256]{3,2,1,0:T(8,128)} %copy.83), kind=kOutput, calls=%fused_computation.37 | convolution fusion | flops 5436407808 | bytes 12582912 | tf_op jit(solution)/shard_map/dot_general | solution.py:76
  261.3 3.5 copy.86
  264.9 8.1 %copy.87 = f32[6,9,128,256]{3,2,1,0:T(8,128)} copy(f32[6,9,128,256]{2,3,0,1:T(8,128)} %get-tuple-element.22) | data formatting | bytes 14155776 | tf_op jit(solution)/shard_map/slice | solution.py:77
  273.0 9.0 %bitcast_multiply_fusion.1 = f32[9,128,512]{2,1,0:T(8,128)S(1)} fusion(f32[8,512,256]{1,2,0:T(8,128)} %reshape.545, f32[6,9,128,256]{3,2,1,0:T(8,128)} %copy.87), kind=kOutput, calls=%fused_computation.36 | convolution fusion | flops 5436407808 | bytes 12582912 | tf_op jit(solution)/shard_map/dot_general | solution.py:76
  282.0 3.5 copy.90
  285.5 8.1 %copy.91 = f32[6,9,128,256]{3,2,1,0:T(8,128)} copy(f32[6,9,128,256]{2,3,0,1:T(8,128)} %get-tuple-element.21) | data formatting | bytes 14155776 | tf_op jit(solution)/shard_map/slice | solution.py:77
  293.6 9.0 %bitcast_multiply_fusion = f32[9,128,512]{2,1,0:T(8,128)S(1)} fusion(f32[8,512,256]{1,2,0:T(8,128)} %reshape.545, f32[6,9,128,256]{3,2,1,0:T(8,128)} %copy.91), kind=kOutput, calls=%fused_computation.35 | convolution fusion | flops 5436407808 | bytes 12582912 | tf_op jit(solution)/shard_map/dot_general | solution.py:76
  302.6 3.6 copy.94
  306.3 4.9 slice_bitcast_fusion.1
  311.2 23.4 %fusion.24 = f32[1152,6,256]{0,2,1:T(8,128)S(1)} fusion(f32[3,1152,512,1]{2,1,0,3:T(8,128)} %bitcast.264, f32[1,6,512,256]{2,3,0,1:T(8,128)S(1)} %get-tuple-element.59, f32[1,6,512,256]{2,3,0,1:T(8,128)S(1)} %get-tuple-element.60, f32[1,6,512,256]{2,3,0,1:T(8,128)S(1)} %get-tuple-element.58), kind=kOutput, calls=%fused_computation.24 | convolution fusion | flops 16312172544 | bytes 23592960 | tf_op jit(solution)/shard_map/dot_general | solution.py:54
  338.0 62.6 %reduce-scatter.15.cloned.1.call-done = f32[9,128,64]{1,0,2:T(8,128)} async-done(((f32[9,128,512]{1,0,2:T(8,128)}), f32[9,128,64]{1,0,2:T(8,128)}) %reduce-scatter.15.cloned.1.call-update) | async-done | bytes 294928 | tf_op jit(solution)/shard_map/reduce_scatter | solution.py:88
  400.6 91.4 %reduce-scatter.17.cloned.1.call-done = f32[9,128,64]{1,0,2:T(8,128)} async-done(((f32[9,128,512]{1,0,2:T(8,128)}), f32[9,128,64]{1,0,2:T(8,128)}) %reduce-scatter.17.cloned.1.call-update) | async-done | bytes 294928 | tf_op jit(solution)/shard_map/reduce_scatter | solution.py:88
  495.0 88.5 %reduce-scatter.7.cloned.1.call-done = f32[9,128,64]{1,0,2:T(8,128)} async-done(((f32[9,128,512]{1,0,2:T(8,128)}), f32[9,128,64]{1,0,2:T(8,128)}) %reduce-scatter.7.cloned.1.call-update) | async-done | bytes 294928 | tf_op jit(solution)/shard_map/reduce_scatter | solution.py:88
  583.5 91.6 %reduce-scatter.9.cloned.1.call-done = f32[9,128,64]{1,0,2:T(8,128)} async-done(((f32[9,128,512]{1,0,2:T(8,128)}), f32[9,128,64]{1,0,2:T(8,128)}) %reduce-scatter.9.cloned.1.call-update) | async-done | bytes 294928 | tf_op jit(solution)/shard_map/reduce_scatter | solution.py:88
  675.1 91.6 %reduce-scatter.11.cloned.1.call-done = f32[9,128,64]{1,0,2:T(8,128)} async-done(((f32[9,128,512]{1,0,2:T(8,128)}), f32[9,128,64]{1,0,2:T(8,128)}) %reduce-scatter.11.cloned.1.call-update) | async-done | bytes 294928 | tf_op jit(solution)/shard_map/reduce_scatter | solution.py:88
  (134 shorter events, 51.4 us)
Async XLA Ops:
  7.2 16.0 %copy-start.10 = (f32[128,6,256]{2,0,1:T(8,128)S(1)}, f32[128,6,256]{2,0,1:T(8,128)}, u32[]{:S(2)}) copy-start(f32[128,6,256]{2,0,1:T(8,128)} %param.7) | copy-start | bytes 2359300
  7.2 49.6 %all-gather.5.cloned.1.call-start = ((), (), s32[]{:S(2)}) async-start(), calls=%async_computation.12 | async-start | bytes 5242880 | tf_op jit(solution)/shard_map/all_gather | solution.py:45
  10.4 7.1 collective-permute-start
  13.8 7.8 collective-permute-start.1
  23.1 183.7 %all-gather.7.cloned.1.call-start = ((), (), s32[]{:S(2)}) async-start(), calls=%async_computation.13 | async-start | bytes 5242880 | tf_op jit(solution)/shard_map/all_gather | solution.py:45
  23.4 3.3 copy-start.4
  23.7 13.4 %collective-permute-start.4 = (f32[1,128,256]{1,2,0:T(8,128)S(1)}, f32[1,128,256]{1,2,0:T(8,128)S(1)}, u32[]{:S(2)}, u32[]{:S(2)}) collective-permute-start(f32[1,128,256]{1,2,0:T(8,128)S(1)} %get-tuple-element.98), channel_id=1, source_target_pairs={{0,4},{4,8},{8,12},{12,16},{16,20},{20,24},{24,28},{1,5},{5,9},{9,... | collective-permute-start | bytes 393224 | tf_op jit(solution)/shard_map/ppermute | solution.py:16
  26.8 10.3 %collective-permute-start.5 = (f32[1,128,256]{1,2,0:T(8,128)S(1)}, f32[1,128,256]{1,2,0:T(8,128)S(1)}, u32[]{:S(2)}, u32[]{:S(2)}) collective-permute-start(f32[1,128,256]{1,2,0:T(8,128)S(1)} %get-tuple-element.99), channel_id=1, source_target_pairs={{4,0},{8,4},{12,8},{16,12},{20,16},{24,20},{28,24},{5,1},{9,5},{13... | collective-permute-start | bytes 393224 | tf_op jit(solution)/shard_map/ppermute | solution.py:17
  31.0 6.0 copy-start.2
  31.1 6.9 collective-permute-start.6
  35.1 7.8 collective-permute-start.7
  107.7 1.1 copy-start.5
  110.8 7.5 collective-permute-start.2
  114.2 8.2 %collective-permute-start.3 = (f32[1,128,256]{1,2,0:T(8,128)S(1)}, f32[1,128,256]{1,2,0:T(8,128)S(1)}, u32[]{:S(2)}, u32[]{:S(2)}) collective-permute-start(f32[1,128,256]{1,2,0:T(8,128)S(1)} %get-tuple-element.101), channel_id=1, source_target_pairs={{4,0},{8,4},{12,8},{16,12},{20,16},{24,20},{28,24},{5,1},{9,5},{13... | collective-permute-start | bytes 393224 | tf_op jit(solution)/shard_map/ppermute | solution.py:17
  126.0 212.0 %reduce-scatter.13.cloned.1.call-start = ((), (), s32[]{:S(2)}) async-start(), calls=%async_computation.9 | async-start | bytes 4718592 | tf_op jit(solution)/shard_map/reduce_scatter | solution.py:88
  126.0 0.8 copy-start.16
  126.1 0.9 copy-start.17
  128.6 3.1 copy-start.3
  129.0 5.5 copy-start.14
  129.0 5.5 copy-start.15
  130.7 5.4 copy-start.8
  130.7 5.4 copy-start.9
  130.7 5.4 copy-start.12
  130.7 5.4 copy-start.13
  131.7 6.1 copy-start.6
  131.8 6.1 copy-start.7
  131.8 6.1 copy-start.11
  181.0 18.6 %slice-start = ((s8[7077888]{0:T(1024)(128)(4,1)}), s8[4194304]{0:T(1024)(128)(4,1)S(1)}, s32[]{:S(2)}) async-start(s8[7077888]{0:T(1024)(128)(4,1)} %bitcast.255), calls=%async_computation.14 | async-start | bytes 8388608
  190.1 9.5 %slice-start.1 = ((s8[7077888]{0:T(1024)(128)(4,1)}), s8[2883584]{0:T(1024)(128)(4,1)S(1)}, s32[]{:S(2)}) async-start(s8[7077888]{0:T(1024)(128)(4,1)} %bitcast.255), calls=%async_computation.15 | async-start | bytes 5767168
  206.8 10.8 %copy-start.1 = (f32[9,128,512]{2,1,0:T(8,128)S(1)}, f32[9,128,512]{2,1,0:T(8,128)}, u32[]{:S(2)}) copy-start(f32[9,128,512]{2,1,0:T(8,128)} %bitcast_multiply_fusion.5) | copy-start | bytes 7077892
  221.0 5.2 copy-start
  221.1 179.5 %reduce-scatter.15.cloned.1.call-start = ((), (), s32[]{:S(2)}) async-start(), calls=%async_computation.10 | async-start | bytes 4718592 | tf_op jit(solution)/shard_map/reduce_scatter | solution.py:88
  226.2 265.8 %reduce-scatter.17.cloned.1.call-start = ((), (), s32[]{:S(2)}) async-start(), calls=%async_computation.11 | async-start | bytes 4718592 | tf_op jit(solution)/shard_map/reduce_scatter | solution.py:88
  229.7 353.7 %reduce-scatter.7.cloned.1.call-start = ((), (), s32[]{:S(2)}) async-start(), calls=%async_computation.6 | async-start | bytes 4718592 | tf_op jit(solution)/shard_map/reduce_scatter | solution.py:88
  264.8 410.2 %reduce-scatter.9.cloned.1.call-start = ((), (), s32[]{:S(2)}) async-start(), calls=%async_computation.7 | async-start | bytes 4718592 | tf_op jit(solution)/shard_map/reduce_scatter | solution.py:88
  285.5 481.2 %reduce-scatter.11.cloned.1.call-start = ((), (), s32[]{:S(2)}) async-start(), calls=%async_computation.8 | async-start | bytes 4718592 | tf_op jit(solution)/shard_map/reduce_scatter | solution.py:88
Sparse Core Ops, SparseCore 0:
  23.2 33.5 all-gather.4
  126.1 33.5 all-gather.6
  221.2 87.9 reduce-scatter.12
  312.6 87.9 reduce-scatter.14
  404.1 87.9 reduce-scatter.16
  495.5 87.9 reduce-scatter.6
  587.1 87.9 reduce-scatter.8
  678.7 87.9 reduce-scatter.10
